TPU v7x, 32 devices: a whole 2x2x4 slice. The times are simulated.
32 devices in a mesh: rep: 4 (over x, y), dp: 8 (over z, core).
Axes of the slice: x: 2, y: 2, z: 4, core: 2. Of those that a mesh axis runs over, the one named last changes fastest.
Arguments:
- x: bfloat16 [32, 2048, 640], P(('rep', 'dp')), parts along dimension 0
- dy: bfloat16 [32, 2048, 640], P(('rep', 'dp')), parts along dimension 0
- w_gate: bfloat16 [2, 640, 2048], replicated
- w_up: bfloat16 [2, 640, 2048], replicated
- w_down: bfloat16 [2, 2048, 640], replicated
- m_w_gate: float32 [2, 640, 2048], replicated
- m_w_up: float32 [2, 640, 2048], replicated
- m_w_down: float32 [2, 2048, 640], replicated
- v_w_gate: float32 [2, 640, 2048], replicated
- v_w_up: float32 [2, 640, 2048], replicated
- v_w_down: float32 [2, 2048, 640], replicated
Outputs:
- output 1: bfloat16 [8, 640, 2048], P('rep'), parts along dimension 0
- output 2: bfloat16 [8, 640, 2048], P('rep'), parts along dimension 0
- output 3: bfloat16 [8, 2048, 640], P('rep'), parts along dimension 0
- output 4: float32 [8, 640, 2048], P('rep'), parts along dimension 0
- output 5: float32 [8, 640, 2048], P('rep'), parts along dimension 0
- output 6: float32 [8, 2048, 640], P('rep'), parts along dimension 0
- output 7: float32 [8, 640, 2048], P('rep'), parts along dimension 0
- output 8: float32 [8, 640, 2048], P('rep'), parts along dimension 0
- output 9: float32 [8, 2048, 640], P('rep'), parts along dimension 0
There are 4 independent parts. A program takes and returns all parts, laid end to end along the dimension named above; an argument that names none is the same for every part.
All inputs are finite; a program needn't handle non-finite values.
Results may differ from a plain program's by a relative error of at most 0.022.
Values are sent between devices in bfloat16 or wider.
A program may use at most 2.25 GiB of HBM per device.

v0:
```python
import jax
import jax.numpy as jnp
from jax import lax
from jax.sharding import PartitionSpec as P

NAMES = ("w_gate", "w_up", "w_down")


def matmul(a, w):
    return jnp.dot(a, w, preferred_element_type=jnp.float32).astype(jnp.bfloat16)


def normed(h):
    wide = h.astype(jnp.float32)
    scale = lax.rsqrt(jnp.mean(wide**2, -1, keepdims=True) + 1e-6)
    return (wide * scale).astype(jnp.bfloat16)


def layer(h, w):
    a = normed(h)
    gate = jnp.dot(a, w["w_gate"], preferred_element_type=jnp.float32)
    up = jnp.dot(a, w["w_up"], preferred_element_type=jnp.float32)
    return h + matmul((jax.nn.silu(gate) * up).astype(jnp.bfloat16), w["w_down"])


def adamw(w, m, v, g):
    m = 0.9 * m + 0.1 * g
    v = 0.95 * v + 0.05 * g * g
    step = m * lax.rsqrt(v + 1e-8) + 0.1 * w
    return (w - 0.02 * step).astype(jnp.bfloat16), m, v


def clipped(gradients, sum_of_squares, count):
    factor = jnp.minimum(1.0, 0.5 * lax.rsqrt(sum_of_squares / count + 1e-30))
    return [g * factor for g in gradients]


def solution(mesh):
    def step(x, dy, *arrays):
        weights, m, v = (arrays[i : i + 3] for i in (0, 3, 6))
        layers = weights[0].shape[0]
        h, kept = x[0], []
        for number in range(layers):
            kept.append(h)
            h = layer(h, {name: w[number] for name, w in zip(NAMES, weights, strict=True)})
        by_h, summed = dy[0], [None] * layers
        for number in reversed(range(layers)):
            _, back = jax.vjp(lambda w, h: layer(h, w), {name: w[number] for name, w in zip(NAMES, weights, strict=True)}, kept[number])
            by_w, by_h = back(by_h)
            summed[number] = [lax.psum(by_w[name], "dp") for name in NAMES]
        gradients = [jnp.stack([summed[number][i] for number in range(layers)]).astype(jnp.float32) for i in range(3)]
        gradients = clipped(gradients, sum(jnp.sum(g * g) for g in gradients), sum(g.size for g in gradients))
        new = [adamw(w.astype(jnp.float32), m, v, g) for w, m, v, g in zip(weights, m, v, gradients, strict=True)]
        return tuple(one[which] for which in range(3) for one in new)

    return jax.shard_map(
        step,
        mesh=mesh,
        in_specs=(P(("rep", "dp"), None, None),) * 2 + (P(None, None, None),) * 9,
        out_specs=(P("rep", None, None),) * 9,
        check_vma=False,
    )
```

profile of v0, /device:TPU:0, one launch (start us, length us, event | category | flops | bytes accessed | tf_op | source)
XLA Modules:
  0.0 617.1 jit_solution(6283104910720893605)
XLA Ops:
  7.2 0.0 all-reduce.3.cloned.1.call-start
  7.2 3.0 copy.20
  10.2 0.0 copy-start.2
  10.2 0.6 fusion.36
  10.8 0.0 copy-start.11
  10.8 4.7 copy.21
  15.5 0.0 copy-start.8
  15.5 11.3 %convolution_convert_fusion.1 = bf16[2048,2048]{1,0:T(8,128)(2,1)} fusion(bf16[1,2048,640]{2,1,0:T(8,128)(2,1)} %param.12, bf16[2,2048,640]{2,1,0:T(8,128)(2,1)} %param.15), kind=kOutput, calls=%fused_computation.65 | convolution fusion | flops 5372903424 | bytes 13631488 | tf_op jit(solution)/shard_map/transpose(jvp())/dot_general | solution.py:10
  26.8 0.0 copy-done.8
  26.8 11.6 %fusion.74 = f32[2048,2048]{1,0:T(8,128)} fusion(bf16[2,640,2048]{2,1,0:T(8,128)(2,1)} %param.13, bf16[1,2048,640]{2,1,0:T(8,128)(2,1)S(1)} %copy-done.8, f32[2048]{0:T(1024)S(1)} %add_rsqrt_fusion), kind=kOutput, calls=%fused_computation.110 | convolution fusion | flops 5372641280 | bytes 22028288 | tf_op jit(solution)/shard_map/dot_general | solution.py:21
  38.4 0.0 copy-done.11
  38.4 16.9 %multiply_convert_fusion.1 = (bf16[2048,2048]{1,0:T(8,128)(2,1)}, f32[2048,2048]{1,0:T(8,128)}) fusion(f32[2048,2048]{1,0:T(8,128)} %fusion.74, bf16[2,640,2048]{2,1,0:T(8,128)(2,1)} %param.14, bf16[1,2048,640]{2,1,0:T(8,128)(2,1)} %param.11, f32[2048]{0:T(1024)S(1)} %add_rsqrt_fusion), kind=kOutput, calls=%fused_computation.17 | convolution fusion | flops 5397807104 | bytes 47194112 | tf_op jit(solution)/shard_map/dot_general | solution.py:22
  55.3 0.0 copy-done.2
  55.3 9.2 %fusion.40 = (f32[2048]{0:T(1024)S(1)}, bf16[2048,640]{0,1:T(8,128)(2,1)S(1)}) fusion(bf16[2048,2048]{1,0:T(8,128)(2,1)} %get-tuple-element.24, bf16[2,2048,640]{2,1,0:T(8,128)(2,1)} %param.15, bf16[1,2048,640]{1,2,0:T(8,128)(2,1)S(1)} %copy.20), kind=kOutput, calls=%fused_computation.73 | convolution fusion | flops 5375260672 | bytes 16261120 | tf_op jit(solution)/shard_map/dot_general | solution.py:10
  64.5 0.0 copy-start.6
  64.5 0.0 copy-start.9
  64.5 1.5 copy-done.6
  66.0 0.0 copy-done.9
  66.0 12.2 %fusion.63 = f32[2048,2048]{1,0:T(8,128)} fusion(bf16[2,640,2048]{2,1,0:T(8,128)(2,1)} %param.14, bf16[2048,640]{0,1:T(8,128)(2,1)S(1)} %get-tuple-element.27, f32[2048]{0:T(1024)S(1)} %fusion.98), kind=kOutput, calls=%fused_computation.99 | convolution fusion | flops 5372641280 | bytes 22028288 | tf_op jit(solution)/shard_map/jvp()/dot_general | solution.py:22
  78.1 0.0 slice-start.2
  78.1 25.1 %fusion.2 = (bf16[2048,2048]{1,0:T(8,128)(2,1)}, f32[2048,2048]{1,0:T(8,128)}) fusion(f32[2048,2048]{1,0:T(8,128)} %fusion.63, bf16[2048,2048]{1,0:T(8,128)(2,1)} %convolution_convert_fusion.1, bf16[2,640,2048]{2,1,0:T(8,128)(2,1)} %param.13, bf16[2048,640]{0,1:T(8,128)(2,1)} %copy-done.6, f32[2048]{0:T(1024)S(1)} %fusion.98), kind=kOutput, calls=%fused_computation.8 | convolution fusion | flops 5422972928 | bytes 55582720 | tf_op jit(solution)/shard_map/jvp()/dot_general | solution.py:21
  103.3 0.0 slice-start.3
  103.3 16.9 %fusion.55 = bf16[1,2048,640]{2,1,0:T(8,128)(2,1)} fusion(f32[2048,2048]{1,0:T(8,128)} %fusion.63, bf16[1,2048,640]{2,1,0:T(8,128)(2,1)} %param.12, f32[2048,2048]{1,0:T(8,128)} %get-tuple-element.29), kind=kOutput, calls=%fused_computation.91 | convolution fusion | flops 5395185664 | bytes 38797312 | tf_op jit(solution)/shard_map/transpose(jvp())/dot_general | solution.py:10
  120.2 0.0 slice-start
  120.2 13.3 %fusion.58 = bf16[1,640,2048]{2,1,0:T(8,128)(2,1)} fusion(bf16[2048,2048]{1,0:T(8,128)(2,1)} %convolution_convert_fusion.1, bf16[2048,640]{0,1:T(8,128)(2,1)} %copy-done.6, f32[2048]{0:T(1024)S(1)} %fusion.98, f32[2048,2048]{1,0:T(8,128)} %get-tuple-element.29), kind=kOutput, calls=%fused_computation.94 | convolution fusion | flops 5399117824 | bytes 30416896 | tf_op jit(solution)/shard_map/transpose(jvp())/dot_general | solution.py:22
  133.5 0.0 slice-done.2
  133.5 0.0 slice-done.3
  133.5 0.0 slice-start.1
  133.5 12.4 %fusion.44 = bf16[2048,640]{0,1:T(8,128)(2,1)} fusion(bf16[2048,2048]{1,0:T(8,128)(2,1)} %convolution_convert_fusion.1, bf16[2,640,2048]{2,1,0:T(8,128)(2,1)S(1)} %bitcast.77, f32[2048,2048]{1,0:T(8,128)} %get-tuple-element.29), kind=kOutput, calls=%fused_computation.81 | convolution fusion | flops 5395185664 | bytes 30408704 | tf_op jit(solution)/shard_map/transpose(jvp())/dot_general | solution.py:22
  145.9 0.0 copy-start.7
  145.9 10.9 %fusion.56 = bf16[1,640,2048]{2,1,0:T(8,128)(2,1)} fusion(bf16[2048,2048]{1,0:T(8,128)(2,1)} %get-tuple-element.28, bf16[2048,640]{0,1:T(8,128)(2,1)} %copy-done.6, f32[2048]{0:T(1024)S(1)} %fusion.98), kind=kOutput, calls=%fused_computation.92 | convolution fusion | flops 5372641280 | bytes 13639680 | tf_op jit(solution)/shard_map/transpose(jvp())/dot_general | solution.py:21
  156.8 0.0 slice-done
  156.8 0.0 slice-done.1
  156.8 0.0 copy-done.7
  156.8 0.0 copy-done.14
  156.9 0.0 copy-start.10
  156.9 0.0 copy-start.1
  156.9 8.5 %fusion.42 = (f32[2048]{0:T(1024)S(1)}, bf16[2048,640]{0,1:T(8,128)(2,1)S(1)}) fusion(bf16[2048,640]{0,1:T(8,128)(2,1)S(1)} %copy-done.7, bf16[2048,640]{0,1:T(8,128)(2,1)S(1)} %copy-done.14, bf16[2048,2048]{1,0:T(8,128)(2,1)} %get-tuple-element.28, bf16[2,640,2048]{2,1,0:T(8,128)(2,1)S(1)} %bitcast.75), kind=kOutput, calls=%fused_computation.75 | convolution fusion | flops 5375260672 | bytes 18882560 | tf_op jit(solution)/shard_map/transpose(jvp())/dot_general | solution.py:21
  165.4 0.0 copy-done.10
  165.4 0.0 copy-done.1
  165.4 0.0 slice-start.4
  165.4 2.0 fusion.60
  167.4 0.0 slice-start.5
  167.5 10.5 %fusion.57 = bf16[1,2048,640]{2,1,0:T(8,128)(2,1)} fusion(bf16[2048,2048]{1,0:T(8,128)(2,1)} %get-tuple-element.24, bf16[2048,640]{0,1:T(8,128)(2,1)S(1)} %fusion.60), kind=kOutput, calls=%fused_computation.93 | convolution fusion | flops 5370019840 | bytes 13631488 | tf_op jit(solution)/shard_map/transpose(jvp())/dot_general | solution.py:10
  177.9 0.0 slice-done.4
  177.9 0.0 slice-done.5
  178.0 0.0 copy-start.12
  178.0 7.3 %convolution_convert_fusion = bf16[2048,2048]{1,0:T(8,128)(2,1)S(1)} fusion(bf16[2048,640]{0,1:T(8,128)(2,1)S(1)} %fusion.60, bf16[2,2048,640]{2,1,0:T(8,128)(2,1)S(1)} %bitcast.79), kind=kOutput, calls=%fused_computation.64 | convolution fusion | flops 5372903424 | bytes 13631488 | tf_op jit(solution)/shard_map/transpose(jvp())/dot_general | solution.py:10
  185.2 0.0 copy-done.3
  185.3 0.0 copy-done.12
  185.3 0.0 copy-start.13
  185.3 13.9 %fusion.51 = bf16[1,640,2048]{2,1,0:T(8,128)(2,1)} fusion(bf16[2048,2048]{1,0:T(8,128)(2,1)S(1)} %convolution_convert_fusion, f32[2048,2048]{1,0:T(8,128)} %fusion.74, bf16[1,2048,640]{1,2,0:T(8,128)(2,1)S(1)} %copy-done.3, f32[2048]{0:T(1024)S(1)} %copy-done.12), kind=kOutput, calls=%fused_computation.89 | convolution fusion | flops 5399117824 | bytes 30416896 | tf_op jit(solution)/shard_map/transpose(jvp())/dot_general | solution.py:22
  199.2 0.0 copy-done.13
  199.2 19.2 %fusion.52 = bf16[1,640,2048]{2,1,0:T(8,128)(2,1)} fusion(f32[2048,2048]{1,0:T(8,128)} %fusion.74, f32[2048,2048]{1,0:T(8,128)} %get-tuple-element.25, bf16[2048,2048]{1,0:T(8,128)(2,1)} %copy-done.13, bf16[1,2048,640]{1,2,0:T(8,128)(2,1)S(1)} %copy-done.3, f32[2048]{0:T(1024)S(1)} %copy-done.12), kind=kOutput, calls=%fused_computation.90 | convolution fusion | flops 5420089344 | bytes 47194112 | tf_op jit(solution)/shard_map/transpose(jvp())/dot_general | solution.py:21
  218.4 0.0 all-reduce.3.cloned.1.call-update
  218.5 316.6 %all-reduce.3.cloned.1.call-done = (bf16[1,640,2048]{2,1,0:T(8,128)(2,1)}, bf16[1,640,2048]{2,1,0:T(8,128)(2,1)}, bf16[1,640,2048]{2,1,0:T(8,128)(2,1)}, bf16[1,...) async-done(((bf16[1,640,2048]{2,1,0:T(8,128)(2,1)}, bf16[1,640,2048]{2,1,0:T(8,128)(2,1)}, bf16[1,640,2048]{2,1,0:T(8,128)(2,1)}, ...) | async-done | bytes 15728656 | tf_op jit(solution)/shard_map/psum | solution.py:50
  535.1 6.0 fusion.24
  541.1 5.8 fusion.23
  546.9 0.0 copy-done.4
  546.9 0.0 copy-done.5
  546.9 3.3 fusion.22
  552.2 0.0 copy-done
  552.2 21.4 %fusion.30 = (bf16[2,2048,640]{2,1,0:T(8,128)(2,1)}, f32[2,2048,640]{2,1,0:T(8,128)}, f32[2,2048,640]{2,1,0:T(8,128)}) fusion(bf16[2,2048,640]{2,1,0:T(8,128)(2,1)} %param.15, f32[]{:T(128)S(6)} %min_shard_map.3, bf16[1,2048,640]{2,1,0:T(8,128)(2,1)S(1)} %copy-done, bf16[1,2048,640]{2,1,0:T(8,128)(2,1)} %get-tuple-element.14, f32[2,2048,640]{2,1,0:T(8,128)} %param.21, ...), kind=kLoop, calls=%fused_computation.54 | loop fusion | flops 52428800 | bytes 57671684 | tf_op jit(solution)/shard_map/convert_element_type | solution.py:30
  573.6 36.1 %fusion.21 = (bf16[2,640,2048]{2,1,0:T(8,128)(2,1)}, f32[2,640,2048]{2,1,0:T(8,128)}, f32[2,640,2048]{2,1,0:T(8,128)}, bf16[2,640,2048]{2,1,0:T(8,128)(2,1)}, f3...) fusion(bf16[2,640,2048]{2,1,0:T(8,128)(2,1)} %param.13, f32[]{:T(128)S(6)} %min_shard_map.3, ...), kind=kLoop, calls=%fused_computation.45 | loop fusion | flops 104857600 | bytes 115343360 | tf_op jit(solution)/shard_map/convert_element_type | solution.py:30
  (11 shorter events, 0.0 us)
Async XLA Ops:
  7.2 527.9 %all-reduce.3.cloned.1.call-start = ((), (), s32[]{:S(2)}) async-start(), calls=%async_computation | async-start | bytes 31457280 | tf_op jit(solution)/shard_map/psum | solution.py:50
  10.2 45.1 %copy-start.2 = (bf16[1,2048,640]{1,2,0:T(8,128)(2,1)}, bf16[1,2048,640]{1,2,0:T(8,128)(2,1)S(1)}, u32[]{:S(2)}) copy-start(bf16[1,2048,640]{1,2,0:T(8,128)(2,1)S(1)} %copy.20) | copy-start | bytes 7864324
  10.8 27.6 %copy-start.11 = (f32[2048]{0:T(1024)}, f32[2048]{0:T(1024)S(1)}, u32[]{:S(2)}) copy-start(f32[2048]{0:T(1024)S(1)} %add_rsqrt_fusion) | copy-start | bytes 24580
  15.5 11.3 %copy-start.8 = (bf16[1,2048,640]{2,1,0:T(8,128)(2,1)S(1)}, bf16[1,2048,640]{2,1,0:T(8,128)(2,1)}, u32[]{:S(2)}) copy-start(bf16[1,2048,640]{2,1,0:T(8,128)(2,1)} %param.11) | copy-start | bytes 7864324
  64.5 1.5 copy-start.6
  64.5 1.5 copy-start.9
  78.1 55.4 %slice-start.2 = ((s8[5242880]{0:T(1024)(128)(4,1)}), s8[1048576]{0:T(1024)(128)(4,1)S(1)}, s32[]{:S(2)}) async-start(s8[5242880]{0:T(1024)(128)(4,1)} %bitcast.76), calls=%async_computation.3 | async-start | bytes 2097152
  103.3 30.2 %slice-start.3 = ((s8[5242880]{0:T(1024)(128)(4,1)}), s8[4194304]{0:T(1024)(128)(4,1)S(1)}, s32[]{:S(2)}) async-start(s8[5242880]{0:T(1024)(128)(4,1)} %bitcast.76), calls=%async_computation.4 | async-start | bytes 8388608
  120.2 36.7 %slice-start = ((s8[5242880]{0:T(1024)(128)(4,1)}), s8[4194304]{0:T(1024)(128)(4,1)S(1)}, s32[]{:S(2)}) async-start(s8[5242880]{0:T(1024)(128)(4,1)} %bitcast.74), calls=%async_computation.1 | async-start | bytes 8388608
  133.5 23.3 %slice-start.1 = ((s8[5242880]{0:T(1024)(128)(4,1)}), s8[1048576]{0:T(1024)(128)(4,1)S(1)}, s32[]{:S(2)}) async-start(s8[5242880]{0:T(1024)(128)(4,1)} %bitcast.74), calls=%async_computation.2 | async-start | bytes 2097152
  145.9 10.9 %copy-start.7 = (bf16[2048,640]{0,1:T(8,128)(2,1)S(1)}, bf16[2048,640]{0,1:T(8,128)(2,1)}, u32[]{:S(2)}) copy-start(bf16[2048,640]{0,1:T(8,128)(2,1)} %copy-done.6) | copy-start | bytes 7864324
  145.9 10.9 %copy-start.14 = (bf16[2048,640]{0,1:T(8,128)(2,1)S(1)}, bf16[2048,640]{0,1:T(8,128)(2,1)}, u32[]{:S(2)}) copy-start(bf16[2048,640]{0,1:T(8,128)(2,1)} %fusion.44) | copy-start | bytes 7864324
  156.9 8.5 %copy-start.10 = (f32[2048]{0:T(1024)S(1)}, f32[2048]{0:T(1024)}, u32[]{:S(2)}) copy-start(f32[2048]{0:T(1024)} %copy-done.9) | copy-start | bytes 24580
  156.9 8.5 %copy-start.1 = (bf16[1,2048,640]{1,2,0:T(8,128)(2,1)S(1)}, bf16[1,2048,640]{1,2,0:T(8,128)(2,1)}, u32[]{:S(2)}) copy-start(bf16[1,2048,640]{1,2,0:T(8,128)(2,1)} %copy.21) | copy-start | bytes 7864324
  165.4 12.5 %slice-start.4 = ((s8[5242880]{0:T(1024)(128)(4,1)}), s8[1048576]{0:T(1024)(128)(4,1)S(1)}, s32[]{:S(2)}) async-start(s8[5242880]{0:T(1024)(128)(4,1)} %bitcast.78), calls=%async_computation.5 | async-start | bytes 2097152
  167.4 10.5 %slice-start.5 = ((s8[5242880]{0:T(1024)(128)(4,1)}), s8[4194304]{0:T(1024)(128)(4,1)S(1)}, s32[]{:S(2)}) async-start(s8[5242880]{0:T(1024)(128)(4,1)} %bitcast.78), calls=%async_computation.6 | async-start | bytes 8388608
  177.9 7.3 %copy-start.3 = (bf16[1,2048,640]{1,2,0:T(8,128)(2,1)S(1)}, bf16[1,2048,640]{1,2,0:T(8,128)(2,1)}, u32[]{:S(2)}) copy-start(bf16[1,2048,640]{1,2,0:T(8,128)(2,1)} %copy-done.2) | copy-start | bytes 7864324
  178.0 7.3 %copy-start.12 = (f32[2048]{0:T(1024)S(1)}, f32[2048]{0:T(1024)}, u32[]{:S(2)}) copy-start(f32[2048]{0:T(1024)} %copy-done.11) | copy-start | bytes 24580
  185.3 13.9 %copy-start.13 = (bf16[2048,2048]{1,0:T(8,128)(2,1)}, bf16[2048,2048]{1,0:T(8,128)(2,1)S(1)}, u32[]{:S(2)}) copy-start(bf16[2048,2048]{1,0:T(8,128)(2,1)S(1)} %convolution_convert_fusion) | copy-start | bytes 25165828
  535.1 11.8 %copy-start.4 = (bf16[1,640,2048]{2,1,0:T(8,128)(2,1)S(1)}, bf16[1,640,2048]{2,1,0:T(8,128)(2,1)}, u32[]{:S(2)}) copy-start(bf16[1,640,2048]{2,1,0:T(8,128)(2,1)} %get-tuple-element.9) | copy-start | bytes 7864324
  535.1 11.8 %copy-start.5 = (bf16[1,640,2048]{2,1,0:T(8,128)(2,1)S(1)}, bf16[1,640,2048]{2,1,0:T(8,128)(2,1)}, u32[]{:S(2)}) copy-start(bf16[1,640,2048]{2,1,0:T(8,128)(2,1)} %get-tuple-element.10) | copy-start | bytes 7864324
  535.1 17.1 %copy-start = (bf16[1,2048,640]{2,1,0:T(8,128)(2,1)S(1)}, bf16[1,2048,640]{2,1,0:T(8,128)(2,1)}, u32[]{:S(2)}) copy-start(bf16[1,2048,640]{2,1,0:T(8,128)(2,1)} %get-tuple-element.13) | copy-start | bytes 7864324
Sparse Core Ops, SparseCore 0:
  218.6 316.4 all-reduce.2
where the time goes:
time: 626 us; the launch traced here: 617 us
  waiting for transfers between devices  317 us (51%)
  matrix products  199 us (32%)
  other arithmetic  75.3 us (12%)
  between operations  16.7 us (3%)
  local copies, waits for them, and re-layouts  9.26 us (1%)
    psum x1, waiting for transfers between devices, step(): summed[number] = [lax.psum(by_w[name], 'dp') for name in NAMES]  317 us
    dot_general x5, matrix products, layer(): gate = jnp.dot(a, w['w_gate'], preferred_element_type=jnp.float32)  75.4 us
    dot_general x5, matrix products, layer(): up = jnp.dot(a, w['w_up'], preferred_element_type=jnp.float32)  68.7 us
    convert_element_type x2, other arithmetic, adamw(): return ((w - 0.02 * step).astype(jnp.bfloat16), m, v)  57.6 us
    dot_general x5, matrix products, matmul(): jnp.dot(a, w, preferred_element_type=jnp.float32).astype(jnp.bfloat16)  55.1 us
    reduce_sum x3, other arithmetic, step(): jnp.sum(g * g)  15.1 us
  transfers between devices with their start and end apart: 1, of which 1 were waited for; matrix products, arithmetic and copies ran while one was open for 0% of the time, Pallas kernels for 0%

commit v1 on v0

v1 whole, which is shorter than its diff:
```python
import functools

import jax
import jax.numpy as jnp
from jax import lax
from jax.experimental import pallas as pl
from jax.experimental.pallas import tpu as pltpu
from jax.sharding import PartitionSpec as P

NAMES = ("w_gate", "w_up", "w_down")
D, FF, LAYERS = 640, 2048, 2
BLOCK = 256
BLOCKS = FF // BLOCK
SUBS = 2
ROWS = D // 2 // SUBS
K = LAYERS * BLOCKS * SUBS
LAG = 2
MESH = pl.DeviceIdType.MESH


def matmul(a, w):
    return jnp.dot(a, w, preferred_element_type=jnp.float32).astype(jnp.bfloat16)


def normed(h):
    wide = h.astype(jnp.float32)
    scale = lax.rsqrt(jnp.mean(wide**2, -1, keepdims=True) + 1e-6)
    return (wide * scale).astype(jnp.bfloat16)


def layer(h, w):
    a = normed(h)
    gate = jnp.dot(a, w["w_gate"], preferred_element_type=jnp.float32)
    up = jnp.dot(a, w["w_up"], preferred_element_type=jnp.float32)
    return h + matmul((jax.nn.silu(gate) * up).astype(jnp.bfloat16), w["w_down"])


def spot(ref, half, q):
    block = q // SUBS
    rows = pl.ds(pl.multiple_of(half * (D // 2) + (q % SUBS) * ROWS, ROWS), ROWS)
    columns = pl.ds(pl.multiple_of((block % BLOCKS) * BLOCK, BLOCK), BLOCK)
    return ref.at[LAYERS - 1 - block // BLOCKS, :, rows, columns]


def reduce_kernel(terms, total, squares, mine, theirs, running, sq, load, pair_s, pair_r, chain_s, chain_r, back_s, back_r, over_s, over_r, out_s, sq_s, sq_r):
    rep, dp = lax.axis_index("rep"), lax.axis_index("dp")
    z, c = dp // 2, dp % 2
    place = z + c * (3 - 2 * z)
    partner = (rep, z * 2 + 1 - c)
    after = (rep, (z + 1 - 2 * c) * 2 + c)
    before = (rep, (z - 1 + 2 * c) * 2 + c)
    barrier = pltpu.get_barrier_semaphore()

    def greet(device):
        pl.semaphore_signal(barrier, inc=1, device_id=device, device_id_type=MESH)

    def remote(source, target, s, r, device):
        return pltpu.make_async_remote_copy(src_ref=source, dst_ref=target, send_sem=s, recv_sem=r, device_id=device, device_id_type=MESH)

    greet(partner)
    pl.when(place < 3)(lambda: greet(after))
    pl.when(place > 0)(lambda: greet(before))
    inner = (place > 0) & (place < 3)
    pl.when(inner)(lambda: pl.semaphore_wait(barrier, 3))
    pl.when(jnp.logical_not(inner))(lambda: pl.semaphore_wait(barrier, 2))

    def loads(q):
        return [pltpu.make_async_copy(spot(terms, half, q), mine.at[half, q], load.at[half, q]) for half in range(2)]

    def pair(q):
        return remote(mine.at[1 - c, q], theirs.at[q], pair_s, pair_r.at[q], partner)

    def chain(q):
        return remote(running.at[q], running.at[q], chain_s, chain_r.at[q], after)

    def back(q):
        return remote(mine.at[c, q], mine.at[c, q], back_s, back_r.at[q], before)

    def over(q):
        return remote(mine.at[c, q], spot(total, c, q), over_s, over_r, partner)

    def out(q):
        return pltpu.make_async_copy(mine.at[c, q], spot(total, c, q), out_s)

    sq[...] = jnp.zeros_like(sq)

    def finished(q):
        pl.when(place > 0)(lambda: back(q).start())
        over(q).start()
        out(q).start()
        g = mine[c, q].astype(jnp.float32).reshape(3 * ROWS // 8, 8, BLOCK)
        s = jnp.sum(g * g, axis=0)
        sq[c] += s[:, :128] + s[:, 128:]

    def add(q):
        pair(q).wait_recv()
        own = mine[c, q].astype(jnp.float32) + theirs[q].astype(jnp.float32)

        @pl.when(place == 0)
        def _():
            running[q] = own.astype(jnp.bfloat16)

        @pl.when(place > 0)
        def _():
            chain(q).wait_recv()

        @pl.when(inner)
        def _():
            running[q] = (own + running[q].astype(jnp.float32)).astype(jnp.bfloat16)

        @pl.when(place == 3)
        def _():
            mine[c, q] = (own + running[q].astype(jnp.float32)).astype(jnp.bfloat16)
            finished(q)

        pl.when(place < 3)(lambda: chain(q).start())

    def service(i):
        q = i - LAG * place
        pl.when((q >= 0) & (q < K))(lambda: add(q))
        r = i - 3 * LAG - LAG * (3 - place)

        @pl.when((r >= 0) & (r < K) & (place < 3))
        def _():
            back(r).wait_recv()
            finished(r)

    def fetch(q, _):
        for copy in loads(q):
            copy.start()
        return 0

    lax.fori_loop(0, K, fetch, 0)

    def ready(i, _):
        for copy in loads(i):
            copy.wait()
        pair(i).start()
        pl.when(i > 0)(lambda: service(i - 1))
        return 0

    lax.fori_loop(0, K, ready, 0)

    def drain(i, _):
        service(i)
        return 0

    lax.fori_loop(K - 1, K + 6 * LAG, drain, 0)

    exchange = remote(sq.at[c], sq.at[c], sq_s, sq_r, partner)
    exchange.start()
    pltpu.make_async_copy(theirs, theirs, pair_s).wait()
    pl.when(place < 3)(lambda: pltpu.make_async_copy(running, running, chain_s).wait())
    pl.when(place > 0)(lambda: pltpu.make_async_copy(running, running, back_s).wait())
    pltpu.make_async_copy(running, running, over_s).wait()
    pltpu.make_async_copy(running, running, over_r).wait()
    pltpu.make_async_copy(running, running, out_s).wait()
    exchange.wait_send()
    remote(sq.at[1 - c], sq.at[1 - c], sq_s, sq_r, partner).wait_recv()
    squares[...] = sq[...]


def summed(terms):
    piece = (3, ROWS, BLOCK)
    dma = pltpu.SemaphoreType.DMA
    return pl.pallas_call(
        reduce_kernel,
        out_shape=(jax.ShapeDtypeStruct(terms.shape, jnp.bfloat16), jax.ShapeDtypeStruct((2, 8, 128), jnp.float32)),
        in_specs=[pl.BlockSpec(memory_space=pl.ANY)],
        out_specs=(pl.BlockSpec(memory_space=pl.ANY), pl.BlockSpec(memory_space=pltpu.VMEM)),
        scratch_shapes=[
            pltpu.VMEM((2, K, *piece), jnp.bfloat16),
            pltpu.VMEM((K, *piece), jnp.bfloat16),
            pltpu.VMEM((K, *piece), jnp.bfloat16),
            pltpu.VMEM((2, 8, 128), jnp.float32),
            dma((2, K)),
            dma, dma((K,)), dma, dma((K,)), dma, dma((K,)), dma, dma, dma, dma, dma,
        ],
        compiler_params=pltpu.CompilerParams(collective_id=0, has_side_effects=True, vmem_limit_bytes=60 * 2**20),
        name="summed",
    )(terms)


def adamw(w, m, v, g):
    m = 0.9 * m + 0.1 * g
    v = 0.95 * v + 0.05 * g * g
    step = m * lax.rsqrt(v + 1e-8) + 0.1 * w
    return (w - 0.02 * step).astype(jnp.bfloat16), m, v


def step_kernel(squares, g, *refs):
    ins, outs = refs[:9], refs[9:]
    factor = jnp.minimum(1.0, 0.5 * lax.rsqrt(jnp.sum(squares[...]) / (3 * LAYERS * D * FF) + 1e-30))
    for i in range(3):
        gradient = g[0, i].astype(jnp.float32)
        if i == 2:
            gradient = gradient.T
        new = adamw(ins[i][0].astype(jnp.float32), ins[3 + i][0], ins[6 + i][0], gradient * factor)
        for which in range(3):
            outs[3 * which + i][0] = new[which]


def stepped(squares, g, arrays):
    wide = pl.BlockSpec((1, D, BLOCK), lambda l, b: (l, 0, b))
    tall = pl.BlockSpec((1, BLOCK, D), lambda l, b: (l, b, 0))
    three = [wide, wide, tall] * 3
    return pl.pallas_call(
        step_kernel,
        grid=(LAYERS, BLOCKS),
        out_shape=[jax.ShapeDtypeStruct(a.shape, a.dtype) for a in arrays],
        in_specs=[
            pl.BlockSpec((2, 8, 128), lambda l, b: (0, 0, 0)),
            pl.BlockSpec((1, 3, D, BLOCK), lambda l, b: (l, 0, 0, b)),
            *three,
        ],
        out_specs=three,
        compiler_params=pltpu.CompilerParams(vmem_limit_bytes=56 * 2**20),
        name="stepped",
    )(squares, g, *arrays)


def solution(mesh):
    def step(x, dy, *arrays):
        weights = arrays[:3]
        h, kept = x[0], []
        for number in range(LAYERS):
            kept.append(h)
            h = layer(h, {name: w[number] for name, w in zip(NAMES, weights, strict=True)})
        by_h, terms = dy[0], [None] * LAYERS
        for number in reversed(range(LAYERS)):
            _, back = jax.vjp(lambda w, h: layer(h, w), {name: w[number] for name, w in zip(NAMES, weights, strict=True)}, kept[number])
            by_w, by_h = back(by_h)
            terms[number] = jnp.stack([by_w["w_gate"], by_w["w_up"], by_w["w_down"].T])
        g, squares = summed(jnp.stack(terms))
        return tuple(stepped(squares, g, arrays))

    return jax.shard_map(
        step,
        mesh=mesh,
        in_specs=(P(("rep", "dp"), None, None),) * 2 + (P(None, None, None),) * 9,
        out_specs=(P("rep", None, None),) * 9,
        check_vma=False,
    )
```

time: 626 us -> 488 us (0.78)
  waiting for transfers between devices: 317 us -> 0 us
  Pallas kernels: 0 us -> 256 us
  other arithmetic: 75.3 us -> 13.2 us
  between operations: 16.7 us -> 1.3 us
    psum x1 -> x0, waiting for transfers between devices: 317 us -> none  [step(): summed[number] = [lax.psum(by_w[name], 'dp') for name in NAMES]]
    pallas_call x0 -> x2, Pallas kernels: none -> 256 us  [the longest x1 196 us: summed(): pl.pallas_call(reduce_kernel, out_shape=(jax.ShapeDtypeStruct(terms.shape...]
    convert_element_type x2 -> x0, other arithmetic: 57.6 us -> none  [adamw(): return ((w - 0.02 * step).astype(jnp.bfloat16), m, v)]
    reduce_sum x3 -> x0, other arithmetic: 15.1 us -> none  [step(): jnp.sum(g * g)]
    another operation x0 -> x2, other arithmetic: none -> 10.8 us  [step(): g, squares = summed(jnp.stack(terms))]
  transfers between devices with their start and end apart: 1 -> 0, of which waited for: 1 -> 0; matrix products, arithmetic and copies ran while one was open for 0% -> 0% of each run, Pallas kernels for 0% -> 0%
where the time goes in v1:
time: 488 us; the launch traced here: 479 us
  Pallas kernels  256 us (52%)
  matrix products  200 us (41%)
  other arithmetic  13.2 us (3%)
  local copies, waits for them, and re-layouts  9.28 us (2%)
    pallas_call x1, Pallas kernels, summed(): pl.pallas_call(reduce_kernel, out_shape=(jax.ShapeDtypeStruct(terms.shape...  196 us
    dot_general x5, matrix products, layer(): gate = jnp.dot(a, w['w_gate'], preferred_element_type=jnp.float32)  76.7 us
    dot_general x5, matrix products, layer(): up = jnp.dot(a, w['w_up'], preferred_element_type=jnp.float32)  66.8 us
    pallas_call x1, Pallas kernels, stepped(): pl.pallas_call(step_kernel, grid=(LAYERS, BLOCKS), out_shape=[jax.ShapeDt...  59.2 us
    dot_general x5, matrix products, matmul(): jnp.dot(a, w, preferred_element_type=jnp.float32).astype(jnp.bfloat16)  56 us
    another operation x2, other arithmetic, step(): g, squares = summed(jnp.stack(terms))  10.8 us

profile of v1, /device:TPU:0, one launch (start us, length us, event | category | flops | bytes accessed | tf_op | source)
XLA Modules:
  0.0 479.1 jit_solution(11120064890207440125)
XLA Ops:
  0.6 3.0 copy.20
  3.6 0.0 copy-start.1
  3.7 0.6 fusion.15
  4.2 0.0 copy-start.12
  4.2 4.7 copy.21
  8.9 0.0 copy-start.5
  8.9 11.3 %convolution_convert_fusion.1 = bf16[2048,2048]{1,0:T(8,128)(2,1)} fusion(bf16[1,2048,640]{2,1,0:T(8,128)(2,1)} %param.12, bf16[2,2048,640]{2,1,0:T(8,128)(2,1)} %refs_2_.1), kind=kOutput, calls=%fused_computation.32 | convolution fusion | flops 5372903424 | bytes 13631488 | tf_op jit(solution)/shard_map/transpose(jvp())/dot_general | solution.py:22
  20.2 0.0 copy-done.5
  20.2 11.6 %fusion.53 = f32[2048,2048]{1,0:T(8,128)} fusion(bf16[2,640,2048]{2,1,0:T(8,128)(2,1)} %refs_0_.1, bf16[1,2048,640]{2,1,0:T(8,128)(2,1)S(1)} %copy-done.5, f32[2048]{0:T(1024)S(1)} %add_rsqrt_fusion), kind=kOutput, calls=%fused_computation.74 | convolution fusion | flops 5372641280 | bytes 22028288 | tf_op jit(solution)/shard_map/dot_general | solution.py:33
  31.8 0.0 copy-done.12
  31.8 16.9 %multiply_convert_fusion.1 = (bf16[2048,2048]{1,0:T(8,128)(2,1)}, f32[2048,2048]{1,0:T(8,128)}) fusion(f32[2048,2048]{1,0:T(8,128)} %fusion.53, bf16[2,640,2048]{2,1,0:T(8,128)(2,1)} %refs_1_.1, bf16[1,2048,640]{2,1,0:T(8,128)(2,1)} %param.11, f32[2048]{0:T(1024)S(1)} %add_rsqrt_fusion), kind=kOutput, calls=%fused_computation.17 | convolution fusion | flops 5397807104 | bytes 47194112 | tf_op jit(solution)/shard_map/dot_general | solution.py:34
  48.7 0.0 copy-done.1
  48.7 9.2 %fusion.19 = (f32[2048]{0:T(1024)S(1)}, bf16[2048,640]{0,1:T(8,128)(2,1)S(1)}) fusion(bf16[2048,2048]{1,0:T(8,128)(2,1)} %get-tuple-element.13, bf16[2,2048,640]{2,1,0:T(8,128)(2,1)} %refs_2_.1, bf16[1,2048,640]{1,2,0:T(8,128)(2,1)S(1)} %copy.20), kind=kOutput, calls=%fused_computation.40 | convolution fusion | flops 5375260672 | bytes 16261120 | tf_op jit(solution)/shard_map/dot_general | solution.py:22
  57.9 0.0 copy-start.10
  57.9 0.0 copy-start.3
  57.9 0.6 copy-done.10
  58.5 0.9 copy-done.3
  59.4 12.4 %fusion.42 = f32[2048,2048]{1,0:T(8,128)} fusion(bf16[2,640,2048]{2,1,0:T(8,128)(2,1)} %refs_1_.1, bf16[2048,640]{0,1:T(8,128)(2,1)S(1)} %get-tuple-element.16, f32[2048]{0:T(1024)S(1)} %fusion.77), kind=kOutput, calls=%fused_computation.63 | convolution fusion | flops 5372641280 | bytes 22028288 | tf_op jit(solution)/shard_map/jvp()/dot_general | solution.py:34
  71.8 25.0 %fusion.2 = (bf16[2048,2048]{1,0:T(8,128)(2,1)}, f32[2048,2048]{1,0:T(8,128)}) fusion(f32[2048,2048]{1,0:T(8,128)} %fusion.42, bf16[2048,2048]{1,0:T(8,128)(2,1)} %convolution_convert_fusion.1, bf16[2,640,2048]{2,1,0:T(8,128)(2,1)} %refs_0_.1, bf16[2048,640]{0,1:T(8,128)(2,1)} %copy-done.3, f32[2048]{0:T(1024)S(1)} %fusion.77), kind=kOutput, calls=%fused_computation.8 | convolution fusion | flops 5422972928 | bytes 55582720 | tf_op jit(solution)/shard_map/jvp()/dot_general | solution.py:33
  96.8 0.0 copy-start.4
  96.8 16.2 %fusion.37 = bf16[1,640,2048]{2,1,0:T(8,128)(2,1)} fusion(f32[2048,2048]{1,0:T(8,128)} %fusion.42, bf16[1,2048,640]{2,1,0:T(8,128)(2,1)} %param.12, f32[2048,2048]{1,0:T(8,128)} %get-tuple-element.18), kind=kOutput, calls=%fused_computation.58 | convolution fusion | flops 5395185664 | bytes 38797312 | tf_op jit(solution)/shard_map/transpose(jvp())/dot_general | solution.py:22
  113.0 0.0 copy-done.4
  113.0 0.0 slice-start.2
  113.0 10.4 %fusion.35 = bf16[1,640,2048]{2,1,0:T(8,128)(2,1)} fusion(bf16[2048,2048]{1,0:T(8,128)(2,1)} %get-tuple-element.17, bf16[2048,640]{0,1:T(8,128)(2,1)S(1)} %copy-done.4, f32[2048]{0:T(1024)S(1)} %fusion.77), kind=kOutput, calls=%fused_computation.56 | convolution fusion | flops 5372641280 | bytes 13639680 | tf_op jit(solution)/shard_map/transpose(jvp())/dot_general | solution.py:33
  123.4 0.0 slice-start.3
  123.4 0.0 slice-start
  123.4 12.6 %fusion.36 = bf16[1,640,2048]{2,1,0:T(8,128)(2,1)} fusion(bf16[2048,2048]{1,0:T(8,128)(2,1)} %convolution_convert_fusion.1, bf16[2048,640]{0,1:T(8,128)(2,1)S(1)} %copy-done.4, f32[2048]{0:T(1024)S(1)} %fusion.77, f32[2048,2048]{1,0:T(8,128)} %get-tuple-element.18), kind=kOutput, calls=%fused_computation.57 | convolution fusion | flops 5399117824 | bytes 30416896 | tf_op jit(solution)/shard_map/transpose(jvp())/dot_general | solution.py:34
  136.0 0.0 slice-done.2
  136.0 0.0 slice-done.3
  136.0 0.0 slice-start.1
  136.0 12.4 %fusion.23 = bf16[2048,640]{0,1:T(8,128)(2,1)} fusion(bf16[2048,2048]{1,0:T(8,128)(2,1)} %convolution_convert_fusion.1, bf16[2,640,2048]{2,1,0:T(8,128)(2,1)S(1)} %bitcast.83, f32[2048,2048]{1,0:T(8,128)} %get-tuple-element.18), kind=kOutput, calls=%fused_computation.45 | convolution fusion | flops 5395185664 | bytes 30408704 | tf_op jit(solution)/shard_map/transpose(jvp())/dot_general | solution.py:34
  148.4 0.0 slice-done
  148.4 0.0 slice-done.1
  148.4 0.0 copy-start.11
  148.4 0.0 copy-start
  148.4 10.4 %fusion.21 = (f32[2048]{0:T(1024)S(1)}, bf16[2048,640]{0,1:T(8,128)(2,1)S(1)}) fusion(bf16[2048,640]{0,1:T(8,128)(2,1)S(1)} %copy-done.4, bf16[2048,640]{0,1:T(8,128)(2,1)} %fusion.23, bf16[2048,2048]{1,0:T(8,128)(2,1)} %get-tuple-element.17, bf16[2,640,2048]{2,1,0:T(8,128)(2,1)S(1)} %bitcast.81), kind=kOutput, calls=%fused_computation.42 | convolution fusion | flops 5375260672 | bytes 18882560 | tf_op jit(solution)/shard_map/transpose(jvp())/dot_general | solution.py:33
  158.8 0.0 copy-done.11
  158.8 0.0 copy-done
  158.8 0.0 slice-start.4
  158.9 1.8 fusion.39
  160.7 0.0 slice-start.5
  160.7 10.4 %fusion.34 = bf16[1,640,2048]{2,1,0:T(8,128)(2,1)} fusion(bf16[2048,640]{0,1:T(8,128)(2,1)S(1)} %fusion.39, bf16[2048,2048]{1,0:T(8,128)(2,1)} %get-tuple-element.13), kind=kOutput, calls=%fused_computation.55 | convolution fusion | flops 5370019840 | bytes 13631488 | tf_op jit(solution)/shard_map/transpose(jvp())/dot_general | solution.py:22
  171.0 0.0 slice-done.4
  171.0 0.0 slice-done.5
  171.0 0.0 copy-start.2
  171.0 0.0 copy-start.13
  171.1 9.0 %convolution_convert_fusion = bf16[2048,2048]{1,0:T(8,128)(2,1)} fusion(bf16[2048,640]{0,1:T(8,128)(2,1)S(1)} %fusion.39, bf16[2,2048,640]{2,1,0:T(8,128)(2,1)S(1)} %bitcast.85), kind=kOutput, calls=%fused_computation.31 | convolution fusion | flops 5372903424 | bytes 13631488 | tf_op jit(solution)/shard_map/transpose(jvp())/dot_general | solution.py:22
  180.1 0.0 copy-done.2
  180.1 0.0 copy-done.13
  180.1 19.3 %fusion.31 = bf16[1,640,2048]{2,1,0:T(8,128)(2,1)} fusion(f32[2048,2048]{1,0:T(8,128)} %fusion.53, f32[2048,2048]{1,0:T(8,128)} %get-tuple-element.14, bf16[2048,2048]{1,0:T(8,128)(2,1)} %convolution_convert_fusion, bf16[1,2048,640]{1,2,0:T(8,128)(2,1)S(1)} %copy-done.2, f32[2048]{0:T(1024)S(1)} %copy-done.13), kind=kOutput, calls=%fused_computation.54 | convolution fusion | flops 5420089344 | bytes 47194112 | tf_op jit(solution)/shard_map/transpose(jvp())/dot_general | solution.py:33
  199.4 0.0 copy-start.6
  199.4 0.0 copy-start.7
  199.4 0.0 copy-start.8
  199.4 0.0 copy-start.9
  199.4 12.6 %fusion.30 = bf16[1,640,2048]{2,1,0:T(8,128)(2,1)} fusion(bf16[2048,2048]{1,0:T(8,128)(2,1)} %convolution_convert_fusion, f32[2048,2048]{1,0:T(8,128)} %fusion.53, bf16[1,2048,640]{1,2,0:T(8,128)(2,1)S(1)} %copy-done.2, f32[2048]{0:T(1024)S(1)} %copy-done.13), kind=kOutput, calls=%fused_computation.53 | convolution fusion | flops 5399117824 | bytes 30416896 | tf_op jit(solution)/shard_map/transpose(jvp())/dot_general | solution.py:34
  212.0 0.0 copy-done.6
  212.0 0.0 copy-done.7
  212.0 0.0 copy-done.8
  212.0 0.0 copy-done.9
  212.0 4.1 maximum_bitcast_fusion
  216.2 6.7 %pad_maximum_fusion.terms = bf16[2,3,640,2048]{3,2,1,0:T(8,128)(2,1)} fusion(bf16[1,3,640,2048]{3,2,1,0:T(8,128)(2,1)S(1)} %get-tuple-element.22, bf16[1,3,640,2048]{3,2,1,0:T(8,128)(2,1)S(1)} %get-tuple-element.21), kind=kLoop, calls=%fused_computation.20 | loop fusion | flops 7864320 | bytes 31457280 | tf_op jit(solution)/shard_map/stack | solution.py:234
  222.9 196.5 %summed.1 = (bf16[2,3,640,2048]{3,2,1,0:T(8,128)(2,1)}, f32[2,8,128]{2,1,0:T(8,128)}) custom-call(bf16[2,3,640,2048]{3,2,1,0:T(8,128)(2,1)} %pad_maximum_fusion.terms), custom_call_target="tpu_custom_call" | custom-call | tf_op jit(solution)/shard_map/summed/pallas_call | solution.py:166
  419.3 59.2 %stepped.1 = (bf16[2,640,2048]{2,1,0:T(8,128)(2,1)}, bf16[2,640,2048]{2,1,0:T(8,128)(2,1)}, bf16[2,2048,640]{2,1,0:T(8,128)(2,1)}, f32[2,640,2048]{2,1,0:T(8,128...) custom-call(f32[2,8,128]{2,1,0:T(8,128)} %get-tuple-element.11.squar, ...), custom_call_target="tpu_custom_call" | custom-call | tf_op jit(solution)/shard_map/stepped/pallas_call | solution.py:207
  (6 shorter events, 0.0 us)
Async XLA Ops:
  3.6 45.0 %copy-start.1 = (bf16[1,2048,640]{1,2,0:T(8,128)(2,1)}, bf16[1,2048,640]{1,2,0:T(8,128)(2,1)S(1)}, u32[]{:S(2)}) copy-start(bf16[1,2048,640]{1,2,0:T(8,128)(2,1)S(1)} %copy.20) | copy-start | bytes 7864324
  4.2 27.6 %copy-start.12 = (f32[2048]{0:T(1024)}, f32[2048]{0:T(1024)S(1)}, u32[]{:S(2)}) copy-start(f32[2048]{0:T(1024)S(1)} %add_rsqrt_fusion) | copy-start | bytes 24580
  8.9 11.3 %copy-start.5 = (bf16[1,2048,640]{2,1,0:T(8,128)(2,1)S(1)}, bf16[1,2048,640]{2,1,0:T(8,128)(2,1)}, u32[]{:S(2)}) copy-start(bf16[1,2048,640]{2,1,0:T(8,128)(2,1)} %param.11) | copy-start | bytes 7864324
  57.9 0.6 copy-start.10
  57.9 1.5 copy-start.3
  96.8 16.2 %copy-start.4 = (bf16[2048,640]{0,1:T(8,128)(2,1)S(1)}, bf16[2048,640]{0,1:T(8,128)(2,1)}, u32[]{:S(2)}) copy-start(bf16[2048,640]{0,1:T(8,128)(2,1)} %copy-done.3) | copy-start | bytes 7864324
  113.0 22.9 %slice-start.2 = ((s8[5242880]{0:T(1024)(128)(4,1)}), s8[4194304]{0:T(1024)(128)(4,1)S(1)}, s32[]{:S(2)}) async-start(s8[5242880]{0:T(1024)(128)(4,1)} %bitcast.82), calls=%async_computation.2 | async-start | bytes 8388608
  123.4 12.6 %slice-start.3 = ((s8[5242880]{0:T(1024)(128)(4,1)}), s8[1048576]{0:T(1024)(128)(4,1)S(1)}, s32[]{:S(2)}) async-start(s8[5242880]{0:T(1024)(128)(4,1)} %bitcast.82), calls=%async_computation.3 | async-start | bytes 2097152
  123.4 25.0 %slice-start = ((s8[5242880]{0:T(1024)(128)(4,1)}), s8[4194304]{0:T(1024)(128)(4,1)S(1)}, s32[]{:S(2)}) async-start(s8[5242880]{0:T(1024)(128)(4,1)} %bitcast.80), calls=%async_computation | async-start | bytes 8388608
  136.0 12.4 %slice-start.1 = ((s8[5242880]{0:T(1024)(128)(4,1)}), s8[1048576]{0:T(1024)(128)(4,1)S(1)}, s32[]{:S(2)}) async-start(s8[5242880]{0:T(1024)(128)(4,1)} %bitcast.80), calls=%async_computation.1 | async-start | bytes 2097152
  148.4 10.4 %copy-start.11 = (f32[2048]{0:T(1024)S(1)}, f32[2048]{0:T(1024)}, u32[]{:S(2)}) copy-start(f32[2048]{0:T(1024)} %copy-done.10) | copy-start | bytes 24580
  148.4 10.4 %copy-start = (bf16[1,2048,640]{1,2,0:T(8,128)(2,1)S(1)}, bf16[1,2048,640]{1,2,0:T(8,128)(2,1)}, u32[]{:S(2)}) copy-start(bf16[1,2048,640]{1,2,0:T(8,128)(2,1)} %copy.21) | copy-start | bytes 7864324
  158.8 12.2 %slice-start.4 = ((s8[5242880]{0:T(1024)(128)(4,1)}), s8[1048576]{0:T(1024)(128)(4,1)S(1)}, s32[]{:S(2)}) async-start(s8[5242880]{0:T(1024)(128)(4,1)} %bitcast.84), calls=%async_computation.4 | async-start | bytes 2097152
  160.7 10.4 %slice-start.5 = ((s8[5242880]{0:T(1024)(128)(4,1)}), s8[4194304]{0:T(1024)(128)(4,1)S(1)}, s32[]{:S(2)}) async-start(s8[5242880]{0:T(1024)(128)(4,1)} %bitcast.84), calls=%async_computation.5 | async-start | bytes 8388608
  171.0 9.1 %copy-start.2 = (bf16[1,2048,640]{1,2,0:T(8,128)(2,1)S(1)}, bf16[1,2048,640]{1,2,0:T(8,128)(2,1)}, u32[]{:S(2)}) copy-start(bf16[1,2048,640]{1,2,0:T(8,128)(2,1)} %copy-done.1) | copy-start | bytes 7864324
  171.0 9.1 %copy-start.13 = (f32[2048]{0:T(1024)S(1)}, f32[2048]{0:T(1024)}, u32[]{:S(2)}) copy-start(f32[2048]{0:T(1024)} %copy-done.12) | copy-start | bytes 24580
  199.4 12.6 %copy-start.6 = (bf16[1,640,2048]{2,1,0:T(8,128)(2,1)S(1)}, bf16[1,640,2048]{2,1,0:T(8,128)(2,1)}, u32[]{:S(2)}) copy-start(bf16[1,640,2048]{2,1,0:T(8,128)(2,1)} %fusion.37) | copy-start | bytes 7864324
  199.4 12.6 %copy-start.7 = (bf16[1,640,2048]{2,1,0:T(8,128)(2,1)S(1)}, bf16[1,640,2048]{2,1,0:T(8,128)(2,1)}, u32[]{:S(2)}) copy-start(bf16[1,640,2048]{2,1,0:T(8,128)(2,1)} %fusion.35) | copy-start | bytes 7864324
  199.4 12.6 %copy-start.8 = (bf16[1,640,2048]{2,1,0:T(8,128)(2,1)S(1)}, bf16[1,640,2048]{2,1,0:T(8,128)(2,1)}, u32[]{:S(2)}) copy-start(bf16[1,640,2048]{2,1,0:T(8,128)(2,1)} %fusion.36) | copy-start | bytes 7864324
  199.4 12.6 %copy-start.9 = (bf16[1,640,2048]{2,1,0:T(8,128)(2,1)S(1)}, bf16[1,640,2048]{2,1,0:T(8,128)(2,1)}, u32[]{:S(2)}) copy-start(bf16[1,640,2048]{2,1,0:T(8,128)(2,1)} %fusion.34) | copy-start | bytes 7864324

commit v2 on v1

--- a/solution.py
+++ b/solution.py
@@ -1,5 +1,3 @@
-import functools
-
 import jax
 import jax.numpy as jnp
 from jax import lax
@@ -7,32 +5,15 @@
 from jax.experimental.pallas import tpu as pltpu
 from jax.sharding import PartitionSpec as P
 
-NAMES = ("w_gate", "w_up", "w_down")
-D, FF, LAYERS = 640, 2048, 2
+TOKENS, D, FF, LAYERS = 2048, 640, 2048, 2
 BLOCK = 256
 BLOCKS = FF // BLOCK
 SUBS = 2
 ROWS = D // 2 // SUBS
 K = LAYERS * BLOCKS * SUBS
 LAG = 2
+TILE = 512
 MESH = pl.DeviceIdType.MESH
-
-
-def matmul(a, w):
-    return jnp.dot(a, w, preferred_element_type=jnp.float32).astype(jnp.bfloat16)
-
-
-def normed(h):
-    wide = h.astype(jnp.float32)
-    scale = lax.rsqrt(jnp.mean(wide**2, -1, keepdims=True) + 1e-6)
-    return (wide * scale).astype(jnp.bfloat16)
-
-
-def layer(h, w):
-    a = normed(h)
-    gate = jnp.dot(a, w["w_gate"], preferred_element_type=jnp.float32)
-    up = jnp.dot(a, w["w_up"], preferred_element_type=jnp.float32)
-    return h + matmul((jax.nn.silu(gate) * up).astype(jnp.bfloat16), w["w_down"])
 
 
 def spot(ref, half, q):
@@ -42,13 +23,34 @@
     return ref.at[LAYERS - 1 - block // BLOCKS, :, rows, columns]
 
 
-def reduce_kernel(terms, total, squares, mine, theirs, running, sq, load, pair_s, pair_r, chain_s, chain_r, back_s, back_r, over_s, over_r, out_s, sq_s, sq_r):
+def dot(a, b):
+    return jnp.dot(a, b, preferred_element_type=jnp.float32)
+
+
+def dot_t(a, b):
+    return lax.dot_general(a, b, (((1,), (1,)), ((), ())), preferred_element_type=jnp.float32)
+
+
+def half_up(x):
+    return x.astype(jnp.bfloat16)
+
+
+def scale_of(wide):
+    return lax.rsqrt(jnp.mean(wide * wide, -1, keepdims=True) + 1e-6)
+
+
+def train_kernel(
+    x_hbm, dy_hbm, gate_hbm, up_hbm, down_hbm, total, squares,
+    mine, theirs, running, sq, h, a_first, a_last, a_t, dy, dy_t, acc, product, by_gu, w_gu, w_d,
+    w_sem, in_sem, pair_s, pair_r, chain_s, chain_r, back_s, back_r, over_s, over_r, out_s, sq_s, sq_r,
+):
     rep, dp = lax.axis_index("rep"), lax.axis_index("dp")
     z, c = dp // 2, dp % 2
     place = z + c * (3 - 2 * z)
     partner = (rep, z * 2 + 1 - c)
     after = (rep, (z + 1 - 2 * c) * 2 + c)
     before = (rep, (z - 1 + 2 * c) * 2 + c)
+    inner = (place > 0) & (place < 3)
     barrier = pltpu.get_barrier_semaphore()
 
     def greet(device):
@@ -57,15 +59,32 @@
     def remote(source, target, s, r, device):
         return pltpu.make_async_remote_copy(src_ref=source, dst_ref=target, send_sem=s, recv_sem=r, device_id=device, device_id_type=MESH)
 
+    def weights(j):
+        number, slot = (j // BLOCKS) % 2, j % 2
+        columns = pl.ds(pl.multiple_of((j % BLOCKS) * BLOCK, BLOCK), BLOCK)
+        return [
+            pltpu.make_async_copy(gate_hbm.at[number, :, columns], w_gu.at[slot, :, pl.ds(0, BLOCK)], w_sem.at[slot, 0]),
+            pltpu.make_async_copy(up_hbm.at[number, :, columns], w_gu.at[slot, :, pl.ds(BLOCK, BLOCK)], w_sem.at[slot, 1]),
+            pltpu.make_async_copy(down_hbm.at[number, columns, :], w_d.at[slot], w_sem.at[slot, 2]),
+        ]
+
+    def next_weights(j):
+        for copy in weights(j):
+            copy.wait()
+
+        @pl.when(j + 1 < 3 * BLOCKS)
+        def _():
+            for copy in weights(j + 1):
+                copy.start()
+
+    inputs = [pltpu.make_async_copy(x_hbm, h, in_sem.at[0]), pltpu.make_async_copy(dy_hbm, dy, in_sem.at[1])]
+    for copy in inputs + weights(0):
+        copy.start()
     greet(partner)
     pl.when(place < 3)(lambda: greet(after))
     pl.when(place > 0)(lambda: greet(before))
-    inner = (place > 0) & (place < 3)
     pl.when(inner)(lambda: pl.semaphore_wait(barrier, 3))
     pl.when(jnp.logical_not(inner))(lambda: pl.semaphore_wait(barrier, 2))
-
-    def loads(q):
-        return [pltpu.make_async_copy(spot(terms, half, q), mine.at[half, q], load.at[half, q]) for half in range(2)]
 
     def pair(q):
         return remote(mine.at[1 - c, q], theirs.at[q], pair_s, pair_r.at[q], partner)
@@ -98,7 +117,7 @@
 
         @pl.when(place == 0)
         def _():
-            running[q] = own.astype(jnp.bfloat16)
+            running[q] = half_up(own)
 
         @pl.when(place > 0)
         def _():
@@ -106,11 +125,11 @@
 
         @pl.when(inner)
         def _():
-            running[q] = (own + running[q].astype(jnp.float32)).astype(jnp.bfloat16)
+            running[q] = half_up(own + running[q].astype(jnp.float32))
 
         @pl.when(place == 3)
         def _():
-            mine[c, q] = (own + running[q].astype(jnp.float32)).astype(jnp.bfloat16)
+            mine[c, q] = half_up(own + running[q].astype(jnp.float32))
             finished(q)
 
         pl.when(place < 3)(lambda: chain(q).start())
@@ -125,27 +144,113 @@
             back(r).wait_recv()
             finished(r)
 
-    def fetch(q, _):
-        for copy in loads(q):
-            copy.start()
+    def tiles(size, body):
+        def at(t, _):
+            body(pl.ds(pl.multiple_of(t * size, size), size))
+            return 0
+
+        lax.fori_loop(0, TOKENS // size, at, 0)
+
+    for copy in inputs:
+        copy.wait()
+
+    def enter(rows):
+        wide = h[rows, :].astype(jnp.float32)
+        a_first[rows, :] = half_up(wide * scale_of(wide))
+        dy_t[:, rows] = half_up(dy[rows, :].astype(jnp.float32).T)
+        acc[rows, :] = jnp.zeros_like(acc[rows, :])
+
+    tiles(256, enter)
+
+    def forward(j, _):
+        next_weights(j)
+        slot = j % 2
+
+        def body(rows):
+            both = dot(a_first[rows, :], w_gu[slot])
+            gate, up = both[:, :BLOCK], both[:, BLOCK:]
+            sigmoid = 0.5 * jnp.tanh(0.5 * gate) + 0.5
+            acc[rows, :] += dot(half_up(gate * sigmoid * up), w_d[slot])
+
+        tiles(TILE, body)
         return 0
 
-    lax.fori_loop(0, K, fetch, 0)
-
-    def ready(i, _):
-        for copy in loads(i):
-            copy.wait()
-        pair(i).start()
-        pl.when(i > 0)(lambda: service(i - 1))
+    lax.fori_loop(0, BLOCKS, forward, 0)
+
+    def between(rows):
+        wide = h[rows, :].astype(jnp.float32) + half_up(acc[rows, :]).astype(jnp.float32)
+        h[rows, :] = half_up(wide)
+        wide = half_up(wide).astype(jnp.float32)
+        a = wide * scale_of(wide)
+        a_last[rows, :] = half_up(a)
+        a_t[:, rows] = half_up(a.T)
+        acc[rows, :] = jnp.zeros_like(acc[rows, :])
+
+    tiles(256, between)
+
+    def backward(n, last):
+        next_weights(BLOCKS + n)
+        slot = n % 2
+        a = a_last if last else a_first
+
+        def body(rows):
+            both = dot(a[rows, :], w_gu[slot])
+            gate, up = both[:, :BLOCK], both[:, BLOCK:]
+            by_product = half_up(dot_t(dy[rows, :], w_d[slot])).astype(jnp.float32)
+            sigmoid = 0.5 * jnp.tanh(0.5 * gate) + 0.5
+            silu = gate * sigmoid
+            product[rows, :] = half_up(silu * up)
+            by_up = half_up(by_product * silu)
+            by_gate = half_up(by_product * up * (sigmoid + silu * (1.0 - sigmoid)))
+            by_both = jnp.concatenate([by_gate, by_up], axis=1)
+            by_gu[rows, :] = by_both
+            if last:
+                acc[rows, :] += dot_t(by_both, w_gu[slot])
+
+        per = TOKENS // TILE // SUBS
+
+        def part(s, _):
+            for t in range(per):
+                body(pl.ds(pl.multiple_of((s * per + t) * TILE, TILE), TILE))
+            service(SUBS * n - SUBS + s)
+            return 0
+
+        lax.fori_loop(0, SUBS, part, 0)
+
+        def gradient(s, _):
+            rows = pl.ds(pl.multiple_of(s * ROWS, ROWS), ROWS)
+            place_in = mine.at[s // SUBS, SUBS * n + s % SUBS]
+            both = half_up(dot(a_t[rows, :], by_gu[...]))
+            place_in[0] = both[:, :BLOCK]
+            place_in[1] = both[:, BLOCK:]
+            place_in[2] = half_up(dot(dy_t[rows, :], product[...]))
+            return 0
+
+        lax.fori_loop(0, 2 * SUBS, gradient, 0)
+        for s in range(SUBS):
+            pair(SUBS * n + s).start()
         return 0
 
-    lax.fori_loop(0, K, ready, 0)
+    lax.fori_loop(0, BLOCKS, lambda n, _: backward(n, True), 0)
+
+    def turn(rows):
+        wide = h[rows, :].astype(jnp.float32)
+        scale = scale_of(wide)
+        by_a = half_up(acc[rows, :]).astype(jnp.float32)
+        by_wide = by_a * scale - wide * (scale * scale * scale * jnp.mean(by_a * wide, -1, keepdims=True))
+        by_h = dy[rows, :].astype(jnp.float32) + half_up(by_wide).astype(jnp.float32)
+        dy[rows, :] = half_up(by_h)
+        dy_t[:, rows] = half_up(by_h.T)
+        a_t[:, rows] = half_up(a_first[rows, :].astype(jnp.float32).T)
+
+    tiles(256, turn)
+    lax.fori_loop(BLOCKS, 2 * BLOCKS, lambda n, _: backward(n, False), 0)
 
     def drain(i, _):
         service(i)
         return 0
 
-    lax.fori_loop(K - 1, K + 6 * LAG, drain, 0)
+    lax.fori_loop(K - SUBS, K + 6 * LAG, drain, 0)
 
     exchange = remote(sq.at[c], sq.at[c], sq_s, sq_r, partner)
     exchange.start()
@@ -160,25 +265,38 @@
     squares[...] = sq[...]
 
 
-def summed(terms):
+def trained(x, dy, gate, up, down):
     piece = (3, ROWS, BLOCK)
     dma = pltpu.SemaphoreType.DMA
+    half, full = jnp.bfloat16, jnp.float32
+    anywhere = pl.BlockSpec(memory_space=pl.ANY)
     return pl.pallas_call(
-        reduce_kernel,
-        out_shape=(jax.ShapeDtypeStruct(terms.shape, jnp.bfloat16), jax.ShapeDtypeStruct((2, 8, 128), jnp.float32)),
-        in_specs=[pl.BlockSpec(memory_space=pl.ANY)],
-        out_specs=(pl.BlockSpec(memory_space=pl.ANY), pl.BlockSpec(memory_space=pltpu.VMEM)),
+        train_kernel,
+        out_shape=(jax.ShapeDtypeStruct((LAYERS, 3, D, FF), half), jax.ShapeDtypeStruct((2, 8, 128), full)),
+        in_specs=[anywhere] * 5,
+        out_specs=(anywhere, pl.BlockSpec(memory_space=pltpu.VMEM)),
         scratch_shapes=[
-            pltpu.VMEM((2, K, *piece), jnp.bfloat16),
-            pltpu.VMEM((K, *piece), jnp.bfloat16),
-            pltpu.VMEM((K, *piece), jnp.bfloat16),
-            pltpu.VMEM((2, 8, 128), jnp.float32),
-            dma((2, K)),
+            pltpu.VMEM((2, K, *piece), half),
+            pltpu.VMEM((K, *piece), half),
+            pltpu.VMEM((K, *piece), half),
+            pltpu.VMEM((2, 8, 128), full),
+            pltpu.VMEM((TOKENS, D), half),
+            pltpu.VMEM((TOKENS, D), half),
+            pltpu.VMEM((TOKENS, D), half),
+            pltpu.VMEM((D, TOKENS), half),
+            pltpu.VMEM((TOKENS, D), half),
+            pltpu.VMEM((D, TOKENS), half),
+            pltpu.VMEM((TOKENS, D), full),
+            pltpu.VMEM((TOKENS, BLOCK), half),
+            pltpu.VMEM((TOKENS, 2 * BLOCK), half),
+            pltpu.VMEM((2, D, 2 * BLOCK), half),
+            pltpu.VMEM((2, BLOCK, D), half),
+            dma((2, 3)), dma((2,)),
             dma, dma((K,)), dma, dma((K,)), dma, dma((K,)), dma, dma, dma, dma, dma,
         ],
-        compiler_params=pltpu.CompilerParams(collective_id=0, has_side_effects=True, vmem_limit_bytes=60 * 2**20),
-        name="summed",
-    )(terms)
+        compiler_params=pltpu.CompilerParams(collective_id=0, has_side_effects=True, vmem_limit_bytes=67043328),
+        name="trained",
+    )(x, dy, gate, up, down)
 
 
 def adamw(w, m, v, g):
@@ -221,17 +339,7 @@
 
 def solution(mesh):
     def step(x, dy, *arrays):
-        weights = arrays[:3]
-        h, kept = x[0], []
-        for number in range(LAYERS):
-            kept.append(h)
-            h = layer(h, {name: w[number] for name, w in zip(NAMES, weights, strict=True)})
-        by_h, terms = dy[0], [None] * LAYERS
-        for number in reversed(range(LAYERS)):
-            _, back = jax.vjp(lambda w, h: layer(h, w), {name: w[number] for name, w in zip(NAMES, weights, strict=True)}, kept[number])
-            by_w, by_h = back(by_h)
-            terms[number] = jnp.stack([by_w["w_gate"], by_w["w_up"], by_w["w_down"].T])
-        g, squares = summed(jnp.stack(terms))
+        g, squares = trained(x[0], dy[0], *arrays[:3])
         return tuple(stepped(squares, g, arrays))
 
     return jax.shard_map(

time: 488 us -> 318 us (0.65); the launches traced: 479 us -> 318 us
  matrix products: 200 us -> 0 us
  Pallas kernels: 256 us -> 317 us
  other arithmetic: 13.2 us -> 0 us
  local copies, waits for them, and re-layouts: 9.28 us -> 0 us
    dot_general x15 -> x0, matrix products: 200 us -> none  [the longest x5 76.7 us: layer(): gate = jnp.dot(a, w['w_gate'], preferred_element_type=jnp.float32)]
    pallas_call x1, Pallas kernels: 196 us -> 258 us  [trained(): pl.pallas_call(train_kernel, out_shape=(jax.ShapeDtypeStruct((LAYERS, 3,...]
    another operation x2 -> x0, other arithmetic: 10.8 us -> none  [step(): g, squares = summed(jnp.stack(terms))]
    unnamed x42 -> x0, local copies, waits for them, and re-layouts: 9.28 us -> none
where the time goes in v2:
time: 318 us
  Pallas kernels  317 us (100%)
    pallas_call x1, Pallas kernels, trained(): pl.pallas_call(train_kernel, out_shape=(jax.ShapeDtypeStruct((LAYERS, 3,...  258 us
    pallas_call x1, Pallas kernels, stepped(): pl.pallas_call(step_kernel, grid=(LAYERS, BLOCKS), out_shape=[jax.ShapeDt...  59.2 us

profile of v2, /device:TPU:0, one launch (start us, length us, event | category | flops | bytes accessed | tf_op | source)
XLA Modules:
  0.0 318.0 jit_solution(6834939558122061278)
XLA Ops:
  0.6 258.1 %trained.1 = (bf16[2,3,640,2048]{3,2,1,0:T(8,128)(2,1)}, f32[2,8,128]{2,1,0:T(8,128)}) custom-call(bf16[2048,640]{1,0:T(8,128)(2,1)} %bitcast.2, bf16[2048,640]{1,0:T(8,128)(2,1)} %bitcast.3, bf16[2,640,2048]{2,1,0:T(8,128)(2,1)} %refs_0_.1, bf16[2,640,2048]{2,1,0:T(8,128)(2,1)} %refs_1_.1, bf16[2,2048,640]{2,1,0:T(8,128)(2,1)} %refs_2_.1), custom_call_target="tpu_custom_call" | custom-call | tf_op jit(solution)/shard_map/trained/pallas_call | solution.py:273
  258.8 59.2 %stepped.1 = (bf16[2,640,2048]{2,1,0:T(8,128)(2,1)}, bf16[2,640,2048]{2,1,0:T(8,128)(2,1)}, bf16[2,2048,640]{2,1,0:T(8,128)(2,1)}, f32[2,640,2048]{2,1,0:T(8,128...) custom-call(f32[2,8,128]{2,1,0:T(8,128)} %get-tuple-element.11.squar, ...), custom_call_target="tpu_custom_call" | custom-call | tf_op jit(solution)/shard_map/stepped/pallas_call | solution.py:325

commit v3 on v2

--- a/solution.py
+++ b/solution.py
@@ -8,11 +8,13 @@
 TOKENS, D, FF, LAYERS = 2048, 640, 2048, 2
 BLOCK = 256
 BLOCKS = FF // BLOCK
-SUBS = 2
+STEP = 512
+SUBS = 4
+PARTS = 4
 ROWS = D // 2 // SUBS
 K = LAYERS * BLOCKS * SUBS
-LAG = 2
-TILE = 512
+LAG, BACK_LAG = 3, 2
+TILE, FORWARD_TILE = 512, 1024
 MESH = pl.DeviceIdType.MESH
 
 
@@ -137,7 +139,7 @@
     def service(i):
         q = i - LAG * place
         pl.when((q >= 0) & (q < K))(lambda: add(q))
-        r = i - 3 * LAG - LAG * (3 - place)
+        r = i - 3 * LAG - BACK_LAG * (3 - place)
 
         @pl.when((r >= 0) & (r < K) & (place < 3))
         def _():
@@ -157,7 +159,6 @@
     def enter(rows):
         wide = h[rows, :].astype(jnp.float32)
         a_first[rows, :] = half_up(wide * scale_of(wide))
-        dy_t[:, rows] = half_up(dy[rows, :].astype(jnp.float32).T)
         acc[rows, :] = jnp.zeros_like(acc[rows, :])
 
     tiles(256, enter)
@@ -172,7 +173,10 @@
             sigmoid = 0.5 * jnp.tanh(0.5 * gate) + 0.5
             acc[rows, :] += dot(half_up(gate * sigmoid * up), w_d[slot])
 
-        tiles(TILE, body)
+            turned = pl.ds(pl.multiple_of(j * (TOKENS // BLOCKS) + rows.start // BLOCKS, 128), FORWARD_TILE // BLOCKS)
+            dy_t[:, turned] = half_up(dy[turned, :].astype(jnp.float32).T)
+
+        tiles(FORWARD_TILE, body)
         return 0
 
     lax.fori_loop(0, BLOCKS, forward, 0)
@@ -207,26 +211,29 @@
             if last:
                 acc[rows, :] += dot_t(by_both, w_gu[slot])
 
-        per = TOKENS // TILE // SUBS
+        per = TOKENS // TILE // PARTS
 
         def part(s, _):
             for t in range(per):
                 body(pl.ds(pl.multiple_of((s * per + t) * TILE, TILE), TILE))
-            service(SUBS * n - SUBS + s)
+            for t in range(SUBS // PARTS):
+                service(SUBS * (n - 1) + s * (SUBS // PARTS) + t)
             return 0
 
-        lax.fori_loop(0, SUBS, part, 0)
-
-        def gradient(s, _):
-            rows = pl.ds(pl.multiple_of(s * ROWS, ROWS), ROWS)
-            place_in = mine.at[s // SUBS, SUBS * n + s % SUBS]
+        lax.fori_loop(0, PARTS, part, 0)
+
+        def gradient(half, _):
+            rows = pl.ds(pl.multiple_of(half * (D // 2), D // 2), D // 2)
             both = half_up(dot(a_t[rows, :], by_gu[...]))
-            place_in[0] = both[:, :BLOCK]
-            place_in[1] = both[:, BLOCK:]
-            place_in[2] = half_up(dot(dy_t[rows, :], product[...]))
+            down = half_up(dot(dy_t[rows, :], product[...]))
+            for s in range(SUBS):
+                here = slice(s * ROWS, (s + 1) * ROWS)
+                mine[half, SUBS * n + s, 0] = both[here, :BLOCK]
+                mine[half, SUBS * n + s, 1] = both[here, BLOCK:]
+                mine[half, SUBS * n + s, 2] = down[here]
             return 0
 
-        lax.fori_loop(0, 2 * SUBS, gradient, 0)
+        lax.fori_loop(0, 2, gradient, 0)
         for s in range(SUBS):
             pair(SUBS * n + s).start()
         return 0
@@ -250,7 +257,7 @@
         service(i)
         return 0
 
-    lax.fori_loop(K - SUBS, K + 6 * LAG, drain, 0)
+    lax.fori_loop(K - SUBS, K + 3 * (LAG + BACK_LAG), drain, 0)
 
     exchange = remote(sq.at[c], sq.at[c], sq_s, sq_r, partner)
     exchange.start()
@@ -319,16 +326,16 @@
 
 
 def stepped(squares, g, arrays):
-    wide = pl.BlockSpec((1, D, BLOCK), lambda l, b: (l, 0, b))
-    tall = pl.BlockSpec((1, BLOCK, D), lambda l, b: (l, b, 0))
+    wide = pl.BlockSpec((1, D, STEP), lambda l, b: (l, 0, b))
+    tall = pl.BlockSpec((1, STEP, D), lambda l, b: (l, b, 0))
     three = [wide, wide, tall] * 3
     return pl.pallas_call(
         step_kernel,
-        grid=(LAYERS, BLOCKS),
+        grid=(LAYERS, FF // STEP),
         out_shape=[jax.ShapeDtypeStruct(a.shape, a.dtype) for a in arrays],
         in_specs=[
             pl.BlockSpec((2, 8, 128), lambda l, b: (0, 0, 0)),
-            pl.BlockSpec((1, 3, D, BLOCK), lambda l, b: (l, 0, 0, b)),
+            pl.BlockSpec((1, 3, D, STEP), lambda l, b: (l, 0, 0, b)),
             *three,
         ],
         out_specs=three,

time: 318 us -> 302 us (0.950)
  Pallas kernels: 317 us -> 301 us
    pallas_call x1, Pallas kernels: 258 us -> 245 us  [trained(): pl.pallas_call(train_kernel, out_shape=(jax.ShapeDtypeStruct((LAYERS, 3,...]
where the time goes in v3:
time: 302 us
  Pallas kernels  301 us (100%)
    pallas_call x1, Pallas kernels, trained(): pl.pallas_call(train_kernel, out_shape=(jax.ShapeDtypeStruct((LAYERS, 3,...  245 us
    pallas_call x1, Pallas kernels, stepped(): pl.pallas_call(step_kernel, grid=(LAYERS, FF // STEP), out_shape=[jax.Sha...  56.3 us

profile of v3, /device:TPU:0, one launch (start us, length us, event | category | flops | bytes accessed | tf_op | source)
XLA Modules:
  0.0 302.0 jit_solution(17851104415952085171)
XLA Ops:
  0.6 244.9 %trained.1 = (bf16[2,3,640,2048]{3,2,1,0:T(8,128)(2,1)}, f32[2,8,128]{2,1,0:T(8,128)}) custom-call(bf16[2048,640]{1,0:T(8,128)(2,1)} %bitcast.2, bf16[2048,640]{1,0:T(8,128)(2,1)} %bitcast.3, bf16[2,640,2048]{2,1,0:T(8,128)(2,1)} %refs_0_.1, bf16[2,640,2048]{2,1,0:T(8,128)(2,1)} %refs_1_.1, bf16[2,2048,640]{2,1,0:T(8,128)(2,1)} %refs_2_.1), custom_call_target="tpu_custom_call" | custom-call | tf_op jit(solution)/shard_map/trained/pallas_call | solution.py:280
  245.6 56.3 %stepped.1 = (bf16[2,640,2048]{2,1,0:T(8,128)(2,1)}, bf16[2,640,2048]{2,1,0:T(8,128)(2,1)}, bf16[2,2048,640]{2,1,0:T(8,128)(2,1)}, f32[2,640,2048]{2,1,0:T(8,128...) custom-call(f32[2,8,128]{2,1,0:T(8,128)} %get-tuple-element.11.squar, ...), custom_call_target="tpu_custom_call" | custom-call | tf_op jit(solution)/shard_map/stepped/pallas_call | solution.py:332

commit v4 on v3

--- a/solution.py
+++ b/solution.py
@@ -8,7 +8,7 @@
 TOKENS, D, FF, LAYERS = 2048, 640, 2048, 2
 BLOCK = 256
 BLOCKS = FF // BLOCK
-STEP = 512
+STEPS = 4
 SUBS = 4
 PARTS = 4
 ROWS = D // 2 // SUBS
@@ -137,14 +137,15 @@
         pl.when(place < 3)(lambda: chain(q).start())
 
     def service(i):
+        r = i - 3 * LAG - BACK_LAG * (3 - place)
+
+        @pl.when((r >= 0) & (r < K) & (place < 3))
+        def _():
+            back(r).wait_recv()
+            finished(r)
+
         q = i - LAG * place
         pl.when((q >= 0) & (q < K))(lambda: add(q))
-        r = i - 3 * LAG - BACK_LAG * (3 - place)
-
-        @pl.when((r >= 0) & (r < K) & (place < 3))
-        def _():
-            back(r).wait_recv()
-            finished(r)
 
     def tiles(size, body):
         def at(t, _):
@@ -153,15 +154,14 @@
 
         lax.fori_loop(0, TOKENS // size, at, 0)
 
-    for copy in inputs:
-        copy.wait()
-
     def enter(rows):
         wide = h[rows, :].astype(jnp.float32)
         a_first[rows, :] = half_up(wide * scale_of(wide))
         acc[rows, :] = jnp.zeros_like(acc[rows, :])
 
-    tiles(256, enter)
+    inputs[0].wait()
+    tiles(512, enter)
+    inputs[1].wait()
 
     def forward(j, _):
         next_weights(j)
@@ -190,7 +190,7 @@
         a_t[:, rows] = half_up(a.T)
         acc[rows, :] = jnp.zeros_like(acc[rows, :])
 
-    tiles(256, between)
+    tiles(512, between)
 
     def backward(n, last):
         next_weights(BLOCKS + n)
@@ -250,7 +250,7 @@
         dy_t[:, rows] = half_up(by_h.T)
         a_t[:, rows] = half_up(a_first[rows, :].astype(jnp.float32).T)
 
-    tiles(256, turn)
+    tiles(512, turn)
     lax.fori_loop(BLOCKS, 2 * BLOCKS, lambda n, _: backward(n, False), 0)
 
     def drain(i, _):
@@ -313,35 +313,34 @@
     return (w - 0.02 * step).astype(jnp.bfloat16), m, v
 
 
-def step_kernel(squares, g, *refs):
+def step_kernel(squares, g_wide, g_tall, *refs):
     ins, outs = refs[:9], refs[9:]
     factor = jnp.minimum(1.0, 0.5 * lax.rsqrt(jnp.sum(squares[...]) / (3 * LAYERS * D * FF) + 1e-30))
     for i in range(3):
-        gradient = g[0, i].astype(jnp.float32)
-        if i == 2:
-            gradient = gradient.T
+        gradient = g_wide[0, i].astype(jnp.float32) if i < 2 else g_tall[0, 0].astype(jnp.float32).T
         new = adamw(ins[i][0].astype(jnp.float32), ins[3 + i][0], ins[6 + i][0], gradient * factor)
         for which in range(3):
             outs[3 * which + i][0] = new[which]
 
 
 def stepped(squares, g, arrays):
-    wide = pl.BlockSpec((1, D, STEP), lambda l, b: (l, 0, b))
-    tall = pl.BlockSpec((1, STEP, D), lambda l, b: (l, b, 0))
+    wide = pl.BlockSpec((1, D // STEPS, FF), lambda l, b: (l, b, 0))
+    tall = pl.BlockSpec((1, FF // STEPS, D), lambda l, b: (l, b, 0))
     three = [wide, wide, tall] * 3
     return pl.pallas_call(
         step_kernel,
-        grid=(LAYERS, FF // STEP),
+        grid=(LAYERS, STEPS),
         out_shape=[jax.ShapeDtypeStruct(a.shape, a.dtype) for a in arrays],
         in_specs=[
             pl.BlockSpec((2, 8, 128), lambda l, b: (0, 0, 0)),
-            pl.BlockSpec((1, 3, D, STEP), lambda l, b: (l, 0, 0, b)),
+            pl.BlockSpec((1, 2, D // STEPS, FF), lambda l, b: (l, 0, b, 0)),
+            pl.BlockSpec((1, 1, D, FF // STEPS), lambda l, b: (l, 2, 0, b)),
             *three,
         ],
         out_specs=three,
         compiler_params=pltpu.CompilerParams(vmem_limit_bytes=56 * 2**20),
         name="stepped",
-    )(squares, g, *arrays)
+    )(squares, g, g, *arrays)
 
 
 def solution(mesh):

time: 302 us -> 299 us (0.990)
  no operation moved by 1% of the time
where the time goes in v4:
time: 299 us
  Pallas kernels  298 us (100%)
    pallas_call x1, Pallas kernels, trained(): pl.pallas_call(train_kernel, out_shape=(jax.ShapeDtypeStruct((LAYERS, 3,...  242 us
    pallas_call x1, Pallas kernels, stepped(): pl.pallas_call(step_kernel, grid=(LAYERS, STEPS), out_shape=[jax.ShapeDty...  55.9 us

profile of v4, /device:TPU:0, one launch (start us, length us, event | category | flops | bytes accessed | tf_op | source)
XLA Modules:
  0.0 299.2 jit_solution(5143446742982738742)
XLA Ops:
  0.6 242.5 %trained.1 = (bf16[2,3,640,2048]{3,2,1,0:T(8,128)(2,1)}, f32[2,8,128]{2,1,0:T(8,128)}) custom-call(bf16[2048,640]{1,0:T(8,128)(2,1)} %bitcast.2, bf16[2048,640]{1,0:T(8,128)(2,1)} %bitcast.3, bf16[2,640,2048]{2,1,0:T(8,128)(2,1)} %refs_0_.1, bf16[2,640,2048]{2,1,0:T(8,128)(2,1)} %refs_1_.1, bf16[2,2048,640]{2,1,0:T(8,128)(2,1)} %refs_2_.1), custom_call_target="tpu_custom_call" | custom-call | tf_op jit(solution)/shard_map/trained/pallas_call | solution.py:280
  243.1 55.9 %stepped.1 = (bf16[2,640,2048]{2,1,0:T(8,128)(2,1)}, bf16[2,640,2048]{2,1,0:T(8,128)(2,1)}, bf16[2,2048,640]{2,1,0:T(8,128)(2,1)}, f32[2,640,2048]{2,1,0:T(8,128...) custom-call(f32[2,8,128]{2,1,0:T(8,128)} %get-tuple-element.11.squar, ...), custom_call_target="tpu_custom_call" | custom-call | tf_op jit(solution)/shard_map/stepped/pallas_call | solution.py:330
